TPU v7x, 32 devices: a whole 2x2x4 slice. The times are simulated.
32 devices in a mesh: grp: 16 (over z, y, core), dom: 2 (over x).
Axes of the slice: x: 2, y: 2, z: 4, core: 2. Of those that a mesh axis runs over, the one named last changes fastest.
Arguments:
- grids: float32 [32, 8, 64, 256], P('grp', None, None, 'dom'), may hold values from -6 to 6
- table: int32 [32, 8], P('grp'), may hold values from 0 to 15, all different within a row
- coefs: int32 [32], P('grp'), may hold values from -10 to 10, as said below
Outputs:
- combined: float32 [32, 8, 64, 256], P('grp', None, None, 'dom')
Inputs may be any that keep to these rules, and one draw needn't show every extreme that they name: The 8 entries of a row of table differ, and every subspace is named by some row. `coefs`: every coefficient is one of 1, -5, 10, -10, 5, -1.
All inputs are finite; a program needn't handle non-finite values.
Results may differ from a plain program's by a relative error of at most 0.00007.
Values sent between devices are 32-bit elements; how exact they have to be, the bound alone decides.
A program may use at most 64 MiB of HBM per device.

v0:
```python
import jax
import jax.numpy as jnp
from jax import lax
from jax.sharding import PartitionSpec as P

SUB_DEV = 1


def on_device(grids, table, coefs):
    local_grids, slots, fields, points = grids.shape
    count = local_grids * slots
    data = grids.reshape(count, fields * points)
    weight = jnp.repeat(coefs.astype(jnp.float32), slots)
    labels = table.reshape(count)
    total_subs = SUB_DEV * lax.axis_size("grp")
    subs_ids = jnp.arange(total_subs, dtype=jnp.int32)
    onehot = (labels[None, :] == subs_ids[:, None]).astype(jnp.float32) * weight[None, :]
    partial_sum = jnp.dot(
        onehot, data, precision=lax.Precision.HIGHEST, preferred_element_type=jnp.float32
    )
    sparse = lax.psum(partial_sum, "grp")
    picker = (labels[:, None] == subs_ids[None, :]).astype(jnp.float32)
    result = jnp.dot(
        picker, sparse, precision=lax.Precision.HIGHEST, preferred_element_type=jnp.float32
    )
    return result.reshape(local_grids, slots, fields, points)


def solution(mesh):
    return jax.shard_map(
        on_device,
        mesh=mesh,
        in_specs=(P("grp", None, None, "dom"), P("grp", None), P("grp")),
        out_specs=P("grp", None, None, "dom"),
        check_vma=False,
    )
```

profile of v0, /device:TPU:0, one launch (start us, length us, event | category | flops | bytes accessed | tf_op | source)
XLA Modules:
  0.0 113.4 jit_solution(12269493009731187399)
XLA Ops:
  6.5 0.0 copy-start
  6.5 0.0 all-reduce.2.cloned.1.call-start
  6.5 0.8 eq.28
  7.3 0.0 copy-done
  7.3 0.1 broadcast_in_dim.2
  7.4 0.1 mul.10
  7.5 2.6 %fusion = f32[16,8192]{1,0:T(8,128)} fusion(f32[2,8,64,128]{3,2,1,0:T(8,128)} %param.3, f32[16]{0:T(128)S(1)} %mul.10, s32[16]{0:T(128)S(1)} %eq.28), kind=kOutput, calls=%fused_computation.1 | convolution fusion | flops 25166336 | bytes 1048704 | tf_op jit(solution)/shard_map/dot_general | solution.py:18
  10.1 0.0 all-reduce.2.cloned.1.call-update
  10.1 94.1 %all-reduce.2.cloned.1.call-done = f32[16,8192]{1,0:T(8,128)} async-done(((f32[16,8192]{1,0:T(8,128)}), f32[16,8192]{1,0:T(8,128)}) %all-reduce.2.cloned.1.call-update) | async-done | bytes 524304 | tf_op jit(solution)/shard_map/psum | solution.py:21
  104.2 1.5 %convolution_bitcast_fusion = f32[2,8,64,128]{3,1,2,0:T(8,128)S(1)} fusion(f32[16,8192]{1,0:T(8,128)} %all-reduce.2.cloned.1.call-done, s32[16]{0:T(128)S(1)} %eq.28), kind=kOutput, calls=%fused_computation | convolution fusion | flops 25166080 | bytes 1048640 | tf_op jit(solution)/shard_map/dot_general | solution.py:23
  105.7 0.9 copy.4
  (1 shorter events, 0.0 us)
Async XLA Ops:
  6.5 0.8 copy-start
  6.5 97.7 %all-reduce.2.cloned.1.call-start = ((), (), s32[]{:S(2)}) async-start(), calls=%async_computation | async-start | bytes 1048576 | tf_op jit(solution)/shard_map/psum | solution.py:21
Sparse Core Ops, SparseCore 0:
  10.7 93.4 all-reduce.1
where the time goes:
time: 114 us; the launch traced here: 113 us
  waiting for transfers between devices  94.1 us (83%)
  between operations  13.4 us (12%)
  matrix products  4.09 us (4%)
  local copies, waits for them, and re-layouts  1.83 us (2%)
    psum x1, waiting for transfers between devices, on_device(): sparse = lax.psum(partial_sum, 'grp')  94.1 us
    dot_general x1, matrix products, on_device(): jnp.dot(onehot, data, precision=lax.Precision.HIGHEST, preferred_element_...  2.64 us
  transfers between devices with their start and end apart: 1, of which 1 were waited for; matrix products, arithmetic and copies ran while one was open for 0% of the time, Pallas kernels for 0%

commit v1 on v0

v1 whole, which is shorter than its diff:
```python
import functools

import jax
import jax.numpy as jnp
from jax import lax
from jax.experimental import pallas as pl
from jax.experimental.pallas import tpu as pltpu
from jax.sharding import PartitionSpec as P

MESH = pl.DeviceIdType.MESH


def factors(n):
    rest = n // 2
    inner = 1 << ((rest.bit_length() - 1) // 2)
    assert n == 2 * inner * (rest // inner)
    return rest // inner, inner


def reduce_kernel(
    n, outer, inner, table, coefs, grids, full, local, part, from_core, from_inner, from_outer,
    load_sem, core_s, core_r, in_s, in_r, out_s, out_r, gout_s, gout_r, gin_s, gin_r, gcore_s, gcore_r,
):
    count, slots = grids.shape[:2]
    load = pltpu.make_async_copy(grids, local, load_sem)
    load.start()

    me = lax.axis_index("grp")
    core = lax.rem(me, 2)
    a = lax.rem(lax.div(me, 2), inner)
    b = lax.div(me, 2 * inner)

    def ident(ob, oa, oc):
        return (lax.rem(b + ob, outer) * inner + lax.rem(a + oa, inner)) * 2 + lax.rem(core + oc, 2)

    def remote(src, dst, send, recv, ob, oa, oc):
        return pltpu.make_async_remote_copy(
            src_ref=src, dst_ref=dst, send_sem=send, recv_sem=recv,
            device_id={"grp": ident(ob, oa, oc)}, device_id_type=MESH,
        )

    barrier = pltpu.get_barrier_semaphore()
    peers = [(0, 0, 1)] + [(0, oa, 0) for oa in range(1, inner)] + [(ob, 0, 0) for ob in range(1, outer)]
    for peer in peers:
        pl.semaphore_signal(barrier, inc=1, device_id={"grp": ident(*peer)}, device_id_type=MESH)

    order_b = sorted(range(1, outer), key=lambda o: -min(o, outer - o)) + [0]
    order_a = list(range(1, inner)) + [0]
    pieces = [(ob, oa) for ob in order_b for oa in order_a]

    weights = [coefs[g].astype(jnp.float32) for g in range(count)]
    labels = [[table[g, k] for k in range(slots)] for g in range(count)]

    def local_sum(sub):
        total = None
        for g in range(count):
            slot = jnp.int32(0)
            weight = jnp.float32(0)
            for k in range(slots):
                here = labels[g][k] == sub
                slot = jnp.where(here, jnp.int32(k), slot)
                weight = jnp.where(here, weights[g], weight)
            term = local[g, slot] * weight
            total = term if total is None else total + term
        return total

    load.wait()
    started = []

    def start(copy):
        copy.start()
        started.append(copy)

    first = True
    for ob, oa in pieces:
        part[ob, oa, 1] = local_sum(ident(ob, oa, 1))
        if first:
            pl.semaphore_wait(barrier, len(peers))
            first = False
        start(remote(part.at[ob, oa, 1], from_core.at[ob, oa], core_s.at[ob, oa], core_r.at[ob, oa], 0, 0, 1))
    for ob, oa in pieces:
        part[ob, oa, 0] = local_sum(ident(ob, oa, 0))

    for ob, oa in pieces:
        remote(part.at[ob, oa, 1], from_core.at[ob, oa], core_s.at[ob, oa], core_r.at[ob, oa], 0, 0, 1).wait_recv()
        if oa:
            part[ob, oa, 0] = part[ob, oa, 0] + from_core[ob, oa]
            start(remote(part.at[ob, oa, 0], from_inner.at[ob, oa], in_s.at[ob, oa], in_r.at[ob, oa], 0, oa, 0))
    for ob in order_b:
        total = part[ob, 0, 0] + from_core[ob, 0]
        for oa in range(1, inner):
            remote(part.at[ob, oa, 0], from_inner.at[ob, oa], in_s.at[ob, oa], in_r.at[ob, oa], 0, oa, 0).wait_recv()
            total = total + from_inner[ob, oa]
        if ob:
            part[ob, 0, 0] = total
            start(remote(part.at[ob, 0, 0], from_outer.at[ob], out_s.at[ob], out_r.at[ob], ob, 0, 0))
    for ob in order_b[:-1]:
        remote(part.at[ob, 0, 0], from_outer.at[ob], out_s.at[ob], out_r.at[ob], ob, 0, 0).wait_recv()
        total = total + from_outer[ob]
    full[me] = total

    def to_outer(o, chunk):
        return remote(full.at[chunk], full.at[chunk], gout_s.at[o], gout_r.at[o], o, 0, 0)

    def to_inner(ob, oa, chunk):
        return remote(full.at[chunk], full.at[chunk], gin_s.at[ob, oa], gin_r.at[ob, oa], 0, oa, 0)

    def to_core(ob, oa, chunk):
        return remote(full.at[chunk], full.at[chunk], gcore_s.at[ob, oa], gcore_r.at[ob, oa], 0, 0, 1)

    def spread(ob):
        chunk = ident(ob, 0, 0)
        for oa in range(1, inner):
            start(to_inner(ob, oa, chunk))
        start(to_core(ob, 0, chunk))

    for o in order_b[:-1]:
        start(to_outer(o, me))
    spread(0)
    near_first = order_b[:-1][::-1]
    for o in near_first:
        to_outer(o, ident(outer - o, 0, 0)).wait_recv()
        spread(outer - o)
    for ob in [0] + [outer - o for o in near_first]:
        for oa in range(1, inner):
            chunk = ident(ob, inner - oa, 0)
            to_inner(ob, oa, chunk).wait_recv()
            start(to_core(ob, inner - oa, chunk))
    for ob, oa in pieces:
        to_core(ob, oa, ident(ob, oa, 1)).wait_recv()
    for copy in started:
        copy.wait_send()


def pick_kernel(table, full, out, sems):
    count, slots = out.shape[:2]
    copies = []
    for g in range(count):
        for k in range(slots):
            copy = pltpu.make_async_copy(full.at[table[g, k]], out.at[g, k], sems.at[g, k])
            copy.start()
            copies.append(copy)
    for copy in copies:
        copy.wait()


def on_device(grids, table, coefs):
    count, slots, fields, points = grids.shape
    n = lax.axis_size("grp")
    outer, inner = factors(n)
    block = (fields, points)
    dma = pltpu.SemaphoreType.DMA
    smem = pl.BlockSpec(memory_space=pltpu.SMEM)
    vmem = pl.BlockSpec(memory_space=pltpu.VMEM)
    hbm = pl.BlockSpec(memory_space=pl.ANY)
    full = pl.pallas_call(
        functools.partial(reduce_kernel, n, outer, inner),
        out_shape=pltpu.VMEM((n,) + block, jnp.float32),
        in_specs=[smem, smem, hbm],
        out_specs=vmem,
        scratch_shapes=[
            pltpu.VMEM((count, slots) + block, jnp.float32),
            pltpu.VMEM((outer, inner, 2) + block, jnp.float32),
            pltpu.VMEM((outer, inner) + block, jnp.float32),
            pltpu.VMEM((outer, inner) + block, jnp.float32),
            pltpu.VMEM((outer,) + block, jnp.float32),
            dma,
        ]
        + [dma((outer, inner))] * 4
        + [dma((outer,))] * 4
        + [dma((outer, inner))] * 4,
        compiler_params=pltpu.CompilerParams(collective_id=0, has_side_effects=True),
        name="reduce_all",
    )(table, coefs, grids)
    return pl.pallas_call(
        pick_kernel,
        out_shape=jax.ShapeDtypeStruct(grids.shape, jnp.float32),
        in_specs=[smem, vmem],
        out_specs=hbm,
        scratch_shapes=[dma((count, slots))],
        name="pick",
    )(table, pltpu.with_memory_space_constraint(full, pltpu.VMEM))


def solution(mesh):
    return jax.shard_map(
        on_device,
        mesh=mesh,
        in_specs=(P("grp", None, None, "dom"), P("grp", None), P("grp")),
        out_specs=P("grp", None, None, "dom"),
        check_vma=False,
    )
```

time: 114 us -> 25.7 us (0.23)
  waiting for transfers between devices: 94.1 us -> 0 us
  Pallas kernels: 0 us -> 25.5 us
  between operations: 13.4 us -> 0.01 us
  matrix products: 4.09 us -> 0 us
  local copies, waits for them, and re-layouts: 1.83 us -> 0 us
    psum x1 -> x0, waiting for transfers between devices: 94.1 us -> none  [on_device(): sparse = lax.psum(partial_sum, 'grp')]
    pallas_call x0 -> x2, Pallas kernels: none -> 25.5 us  [the longest x1 23.9 us: on_device(): pl.pallas_call(functools.partial(reduce_kernel, n, outer, inner), out_sha...]
    dot_general x2 -> x0, matrix products: 4.09 us -> none  [the longest x1 2.64 us: on_device(): jnp.dot(onehot, data, precision=lax.Precision.HIGHEST, preferred_element_...]
  transfers between devices with their start and end apart: 1 -> 0, of which waited for: 1 -> 0; matrix products, arithmetic and copies ran while one was open for 0% -> 0% of each run, Pallas kernels for 0% -> 0%
where the time goes in v1:
time: 25.7 us; the launch traced here: 25.5 us
  Pallas kernels  25.5 us (99%)
    pallas_call x1, Pallas kernels, on_device(): pl.pallas_call(functools.partial(reduce_kernel, n, outer, inner), out_sha...  23.9 us
    pallas_call x1, Pallas kernels, on_device(): pl.pallas_call(pick_kernel, out_shape=jax.ShapeDtypeStruct(grids.shape, j...  1.61 us

profile of v1, /device:TPU:0, one launch (start us, length us, event | category | flops | bytes accessed | tf_op | source)
XLA Modules:
  0.0 25.5 jit_solution(3720666779896283375)
XLA Ops:
  0.0 23.9 %reduce_all.1.full = f32[16,64,128]{2,1,0:T(8,128)S(1)} custom-call(s32[2,8]{1,0:T(2,128)} %table.3, s32[2]{0:T(128)} %coefs.1, f32[2,8,64,128]{3,2,1,0:T(8,128)} %grids.1), custom_call_target="tpu_custom_call" | custom-call | tf_op jit(solution)/shard_map/reduce_all/pallas_call | solution.py:156
  23.9 1.6 %pick.1 = f32[2,8,64,128]{3,2,1,0:T(8,128)} custom-call(s32[2,8]{1,0:T(2,128)} %table.3, f32[16,64,128]{2,1,0:T(8,128)S(1)} %reduce_all.1.full), custom_call_target="tpu_custom_call" | custom-call | tf_op jit(solution)/shard_map/pick/pallas_call | solution.py:175

commit v2 on v0

v2 whole, which is shorter than its diff:
```python
import functools

import jax
import jax.numpy as jnp
from jax import lax
from jax.experimental import pallas as pl
from jax.experimental.pallas import tpu as pltpu
from jax.sharding import PartitionSpec as P

MESH = pl.DeviceIdType.MESH


def factors(n):
    rest = n // 2
    inner = 1 << ((rest.bit_length() - 1) // 2)
    assert n == 2 * inner * (rest // inner)
    return rest // inner, inner


def reduce_kernel(
    n, outer, inner, spread_by, table, coefs, grids, out, local, part, from_core, from_inner, from_outer, full,
    load_sem, core_s, core_r, in_s, in_r, gin_s, gin_r, gcore_s, gcore_r, out_s, out_r, gout_s, gout_r,
):
    count, slots = grids.shape[:2]
    load = pltpu.make_async_copy(grids, local, load_sem)
    load.start()

    me = lax.axis_index("grp")
    core = lax.rem(me, 2)
    a = lax.rem(lax.div(me, 2), inner)
    b = lax.div(me, 2 * inner)

    owners = outer // spread_by
    base = (outer - owners) // 2
    half = outer // 2
    upper = lax.div(b, max(half, 1)) if half else 0
    is_owner = (b >= base) & (b < base + owners)

    def chunk_at(j):
        return lax.rem((1 - upper) * half + j, outer)

    def position(i):
        return lax.rem(i - (1 - upper) * half + outer, outer)

    def owner(i):
        return base + lax.div(i, spread_by)

    def ident(i, oa, oc):
        return (i * inner + lax.rem(a + oa, inner)) * 2 + lax.rem(core + oc, 2)

    def remote(src, dst, send, recv, device):
        return pltpu.make_async_remote_copy(
            src_ref=src, dst_ref=dst, send_sem=send, recv_sem=recv,
            device_id={"grp": device}, device_id_type=MESH,
        )

    partner = ident(b, 0, 1)

    def outer_peer(d):
        return ident(lax.rem(b + d, outer), 0, 0)

    barrier = pltpu.get_barrier_semaphore()
    peers = [outer_peer(d) for d in range(1, outer)] + [ident(b, oa, 0) for oa in range(1, inner)] + [partner]
    for peer in peers:
        pl.semaphore_signal(barrier, inc=1, device_id={"grp": peer}, device_id_type=MESH)

    order_a = list(range(1, inner)) + [0]
    pieces = [(j, oa) for j in range(outer) for oa in order_a]

    weights = [coefs[g].astype(jnp.float32) for g in range(count)]
    labels = [[table[g, k] for k in range(slots)] for g in range(count)]

    def local_sum(sub):
        total = None
        for g in range(count):
            slot = jnp.int32(0)
            weight = jnp.float32(0)
            for k in range(slots):
                here = labels[g][k] == sub
                slot = jnp.where(here, jnp.int32(k), slot)
                weight = jnp.where(here, weights[g], weight)
            term = local[g, slot] * weight
            total = term if total is None else total + term
        return total

    started = []

    def start(copy, when=None):
        if when is None:
            copy.start()
        else:
            pl.when(when)(copy.start)
        started.append((copy, when))

    def core_copy(j, oa):
        return remote(part.at[j, oa, 1], from_core.at[j, oa], core_s.at[j, oa], core_r.at[j, oa], partner)

    def inner_copy(j, oa):
        return remote(part.at[j, oa, 0], from_inner.at[j, oa], in_s.at[j, oa], in_r.at[j, oa], ident(b, oa, 0))

    def outer_copy(j):
        i = chunk_at(j)
        to = owner(i)
        slot, behind = lax.rem(i, spread_by), lax.rem(b - to + outer, outer)
        return remote(
            part.at[j, 0, 0], from_outer.at[slot, behind], out_s.at[j], out_r.at[slot, behind], ident(to, 0, 0)
        ), to != b

    load.wait()
    for j, oa in pieces:
        part[j, oa, 1] = local_sum(ident(chunk_at(j), oa, 1))
    for j, oa in pieces:
        part[j, oa, 0] = local_sum(ident(chunk_at(j), oa, 0))
    pl.semaphore_wait(barrier, len(peers))
    for j, oa in pieces:
        start(core_copy(j, oa))

    for j, oa in pieces:
        core_copy(j, oa).wait_recv()
        if oa:
            part[j, oa, 0] = part[j, oa, 0] + from_core[j, oa]
            start(inner_copy(j, oa))
    for j in range(outer):
        total = part[j, 0, 0] + from_core[j, 0]
        for oa in range(1, inner):
            inner_copy(j, oa).wait_recv()
            total = total + from_inner[j, oa]
        part[j, 0, 0] = total
        start(*outer_copy(j))

    def from_owner(i, d, send):
        chunk = ident(i, 0, 0)
        return remote(full.at[chunk], full.at[chunk], send, gout_r.at[i], outer_peer(d))

    def to_inner(j, oa, source):
        chunk = ident(chunk_at(j), source, 0)
        return remote(full.at[chunk], full.at[chunk], gin_s.at[j, oa], gin_r.at[j, oa], ident(b, oa, 0))

    def to_core(j, source, oc):
        chunk = ident(chunk_at(j), source, oc)
        return remote(full.at[chunk], full.at[chunk], gcore_s.at[j, source], gcore_r.at[j, source], partner)

    far_first = sorted(range(1, outer), key=lambda d: -min(d, outer - d))
    along = 1 - 2 * upper

    def final(slot):
        i = (b - base) * spread_by + slot
        total = part[position(i), 0, 0]
        for d in range(1, outer):
            remote(
                part.at[0, 0, 0], from_outer.at[slot, d], out_s.at[0], out_r.at[slot, d], outer_peer(d)
            ).wait_recv()
            total = total + from_outer[slot, d]
        full[ident(i, 0, 0)] = total
        for d in far_first:
            from_owner(i, lax.rem(along * d + outer, outer), gout_s.at[slot, d]).start()

    @pl.when(is_owner)
    def _():
        for slot in range(spread_by):
            final(slot)

    near_first = list(range(half, outer)) + list(range(half))
    for j in near_first:
        i = chunk_at(j)

        @pl.when(owner(i) != b)
        def _():
            from_owner(i, 1, gout_s.at[0, 0]).wait_recv()

        for oa in range(1, inner):
            start(to_inner(j, oa, 0))
        start(to_core(j, 0, 0))
    for j in near_first:
        for oa in range(1, inner):
            to_inner(j, oa, inner - oa).wait_recv()
            start(to_core(j, inner - oa, 0))
    for j in near_first:
        for oa in range(inner):
            to_core(j, oa, 1).wait_recv()
    for g in range(count):
        for k in range(slots):
            out[g, k] = full[labels[g][k]]

    for copy, when in started:
        if when is None:
            copy.wait_send()
        else:
            pl.when(when)(copy.wait_send)

    @pl.when(is_owner)
    def _():
        for slot in range(spread_by):
            for d in far_first:
                i = (b - base) * spread_by + slot
                from_owner(i, lax.rem(along * d + outer, outer), gout_s.at[slot, d]).wait_send()


def on_device(grids, table, coefs):
    count, slots, fields, points = grids.shape
    n = lax.axis_size("grp")
    outer, inner = factors(n)
    spread_by = 2 if outer % 4 == 0 else 1
    block = (fields, points)
    dma = pltpu.SemaphoreType.DMA
    smem = pl.BlockSpec(memory_space=pltpu.SMEM)
    return pl.pallas_call(
        functools.partial(reduce_kernel, n, outer, inner, spread_by),
        out_shape=pltpu.VMEM(grids.shape, jnp.float32),
        in_specs=[smem, smem, pl.BlockSpec(memory_space=pl.ANY)],
        out_specs=pl.BlockSpec(memory_space=pltpu.VMEM),
        scratch_shapes=[
            pltpu.VMEM((count, slots) + block, jnp.float32),
            pltpu.VMEM((outer, inner, 2) + block, jnp.float32),
            pltpu.VMEM((outer, inner) + block, jnp.float32),
            pltpu.VMEM((outer, inner) + block, jnp.float32),
            pltpu.VMEM((spread_by, outer) + block, jnp.float32),
            pltpu.VMEM((n,) + block, jnp.float32),
            dma,
        ]
        + [dma((outer, inner))] * 8
        + [dma((outer,)), dma((spread_by, outer)), dma((spread_by, outer)), dma((outer,))],
        compiler_params=pltpu.CompilerParams(collective_id=0, has_side_effects=True),
        name="reduce_all",
    )(table, coefs, grids)


def solution(mesh):
    return jax.shard_map(
        on_device,
        mesh=mesh,
        in_specs=(P("grp", None, None, "dom"), P("grp", None), P("grp")),
        out_specs=P("grp", None, None, "dom"),
        check_vma=False,
    )
```

time: 114 us -> 24.9 us (0.22)
  waiting for transfers between devices: 94.1 us -> 0 us
  Pallas kernels: 0 us -> 23.9 us
  between operations: 13.4 us -> 0.01 us
  matrix products: 4.09 us -> 0 us
    psum x1 -> x0, waiting for transfers between devices: 94.1 us -> none  [on_device(): sparse = lax.psum(partial_sum, 'grp')]
    pallas_call x0 -> x1, Pallas kernels: none -> 23.9 us  [on_device(): pl.pallas_call(functools.partial(reduce_kernel, n, outer, inner, spread_b...]
    dot_general x2 -> x0, matrix products: 4.09 us -> none  [the longest x1 2.64 us: on_device(): jnp.dot(onehot, data, precision=lax.Precision.HIGHEST, preferred_element_...]
  transfers between devices with their start and end apart: 1 -> 0, of which waited for: 1 -> 0; matrix products, arithmetic and copies ran while one was open for 0% -> 0% of each run, Pallas kernels for 0% -> 0%
where the time goes in v2:
time: 24.9 us; the launch traced here: 24.7 us
  Pallas kernels  23.9 us (96%)
  local copies, waits for them, and re-layouts  0.8 us (3%)
    pallas_call x1, Pallas kernels, on_device(): pl.pallas_call(functools.partial(reduce_kernel, n, outer, inner, spread_b...  23.9 us
    unnamed x1, local copies, waits for them, and re-layouts  0.8 us

profile of v2, /device:TPU:0, one launch (start us, length us, event | category | flops | bytes accessed | tf_op | source)
XLA Modules:
  0.0 24.7 jit_solution(1846565708296413040)
XLA Ops:
  0.0 23.9 %reduce_all.1 = f32[2,8,64,128]{3,2,1,0:T(8,128)S(1)} custom-call(s32[2,8]{1,0:T(2,128)} %table.1, s32[2]{0:T(128)} %coefs.1, f32[2,8,64,128]{3,2,1,0:T(8,128)} %grids.1), custom_call_target="tpu_custom_call" | custom-call | tf_op jit(solution)/shard_map/reduce_all/pallas_call | solution.py:207
  23.9 0.8 %copy.5 = f32[2,8,64,128]{3,2,1,0:T(8,128)} copy(f32[2,8,64,128]{3,2,1,0:T(8,128)S(1)} %reduce_all.1) | data formatting | bytes 1048576

commit v3 on v2

--- a/solution.py
+++ b/solution.py
@@ -60,9 +60,20 @@
         return ident(lax.rem(b + d, outer), 0, 0)
 
     barrier = pltpu.get_barrier_semaphore()
-    peers = [outer_peer(d) for d in range(1, outer)] + [ident(b, oa, 0) for oa in range(1, inner)] + [partner]
-    for peer in peers:
+    def signal(peer):
         pl.semaphore_signal(barrier, inc=1, device_id={"grp": peer}, device_id_type=MESH)
+
+    for d in sorted(range(1, outer), key=lambda d: -min(d, outer - d)):
+        to = lax.rem(b + d, outer)
+
+        @pl.when(is_owner | ((to >= base) & (to < base + owners)))
+        def _():
+            signal(ident(to, 0, 0))
+
+    for oa in range(1, inner):
+        signal(ident(b, oa, 0))
+    signal(partner)
+    arrivals = inner + jnp.where(is_owner, outer - 1, owners)
 
     order_a = list(range(1, inner)) + [0]
     pieces = [(j, oa) for j in range(outer) for oa in order_a]
@@ -111,7 +122,7 @@
         part[j, oa, 1] = local_sum(ident(chunk_at(j), oa, 1))
     for j, oa in pieces:
         part[j, oa, 0] = local_sum(ident(chunk_at(j), oa, 0))
-    pl.semaphore_wait(barrier, len(peers))
+    pl.semaphore_wait(barrier, arrivals)
     for j, oa in pieces:
         start(core_copy(j, oa))
 

time: 24.9 us -> 23.7 us (0.952)
  Pallas kernels: 23.9 us -> 22.8 us
    pallas_call x1, Pallas kernels: 23.9 us -> 22.8 us  [on_device(): pl.pallas_call(functools.partial(reduce_kernel, n, outer, inner, spread_b...]
where the time goes in v3:
time: 23.7 us; the launch traced here: 23.6 us
  Pallas kernels  22.8 us (96%)
  local copies, waits for them, and re-layouts  0.8 us (3%)
    pallas_call x1, Pallas kernels, on_device(): pl.pallas_call(functools.partial(reduce_kernel, n, outer, inner, spread_b...  22.8 us
    unnamed x1, local copies, waits for them, and re-layouts  0.8 us

profile of v3, /device:TPU:0, one launch (start us, length us, event | category | flops | bytes accessed | tf_op | source)
XLA Modules:
  0.0 23.6 jit_solution(2623493043483360959)
XLA Ops:
  0.0 22.8 %reduce_all.1 = f32[2,8,64,128]{3,2,1,0:T(8,128)S(1)} custom-call(s32[2,8]{1,0:T(2,128)} %table.1, s32[2]{0:T(128)} %coefs.1, f32[2,8,64,128]{3,2,1,0:T(8,128)} %grids.1), custom_call_target="tpu_custom_call" | custom-call | tf_op jit(solution)/shard_map/reduce_all/pallas_call | solution.py:218
  22.8 0.8 %copy.5 = f32[2,8,64,128]{3,2,1,0:T(8,128)} copy(f32[2,8,64,128]{3,2,1,0:T(8,128)S(1)} %reduce_all.1) | data formatting | bytes 1048576

commit v4 on v3

--- a/solution.py
+++ b/solution.py
@@ -18,13 +18,10 @@
 
 
 def reduce_kernel(
-    n, outer, inner, spread_by, table, coefs, grids, out, local, part, from_core, from_inner, from_outer, full,
-    load_sem, core_s, core_r, in_s, in_r, gin_s, gin_r, gcore_s, gcore_r, out_s, out_r, gout_s, gout_r,
+    n, outer, inner, spread_by, table_in, coefs_in, grids, out, table, coefs, local, part, from_core, from_inner, from_outer, full,
+    load_sem, table_sem, coefs_sem, core_s, core_r, in_s, in_r, gin_s, gin_r, gcore_s, gcore_r, out_s, out_r, gout_s, gout_r,
 ):
     count, slots = grids.shape[:2]
-    load = pltpu.make_async_copy(grids, local, load_sem)
-    load.start()
-
     me = lax.axis_index("grp")
     core = lax.rem(me, 2)
     a = lax.rem(lax.div(me, 2), inner)
@@ -75,9 +72,19 @@
     signal(partner)
     arrivals = inner + jnp.where(is_owner, outer - 1, owners)
 
+    loads = [
+        pltpu.make_async_copy(table_in, table, table_sem),
+        pltpu.make_async_copy(coefs_in, coefs, coefs_sem),
+        pltpu.make_async_copy(grids, local, load_sem),
+    ]
+    for load in loads:
+        load.start()
+
     order_a = list(range(1, inner)) + [0]
-    pieces = [(j, oa) for j in range(outer) for oa in order_a]
-
+    pieces = [(j, oa) for oa in order_a for j in range(outer)]
+
+    for load in loads[:2]:
+        load.wait()
     weights = [coefs[g].astype(jnp.float32) for g in range(count)]
     labels = [[table[g, k] for k in range(slots)] for g in range(count)]
 
@@ -117,7 +124,7 @@
             part.at[j, 0, 0], from_outer.at[slot, behind], out_s.at[j], out_r.at[slot, behind], ident(to, 0, 0)
         ), to != b
 
-    load.wait()
+    loads[2].wait()
     for j, oa in pieces:
         part[j, oa, 1] = local_sum(ident(chunk_at(j), oa, 1))
     for j, oa in pieces:
@@ -165,6 +172,9 @@
         full[ident(i, 0, 0)] = total
         for d in far_first:
             from_owner(i, lax.rem(along * d + outer, outer), gout_s.at[slot, d]).start()
+        for oa in range(1, inner):
+            to_inner(position(i), oa, 0).start()
+        to_core(position(i), 0, 0).start()
 
     @pl.when(is_owner)
     def _():
@@ -178,10 +188,13 @@
         @pl.when(owner(i) != b)
         def _():
             from_owner(i, 1, gout_s.at[0, 0]).wait_recv()
-
-        for oa in range(1, inner):
-            start(to_inner(j, oa, 0))
-        start(to_core(j, 0, 0))
+            for oa in range(1, inner):
+                to_inner(j, oa, 0).start()
+            to_core(j, 0, 0).start()
+
+        for oa in range(1, inner):
+            started.append((to_inner(j, oa, 0), None))
+        started.append((to_core(j, 0, 0), None))
     for j in near_first:
         for oa in range(1, inner):
             to_inner(j, oa, inner - oa).wait_recv()
@@ -214,19 +227,22 @@
     spread_by = 2 if outer % 4 == 0 else 1
     block = (fields, points)
     dma = pltpu.SemaphoreType.DMA
-    smem = pl.BlockSpec(memory_space=pltpu.SMEM)
     return pl.pallas_call(
         functools.partial(reduce_kernel, n, outer, inner, spread_by),
         out_shape=pltpu.VMEM(grids.shape, jnp.float32),
-        in_specs=[smem, smem, pl.BlockSpec(memory_space=pl.ANY)],
+        in_specs=[pl.BlockSpec(memory_space=pl.ANY)] * 3,
         out_specs=pl.BlockSpec(memory_space=pltpu.VMEM),
         scratch_shapes=[
+            pltpu.SMEM(table.shape, jnp.int32),
+            pltpu.SMEM(coefs.shape, jnp.int32),
             pltpu.VMEM((count, slots) + block, jnp.float32),
             pltpu.VMEM((outer, inner, 2) + block, jnp.float32),
             pltpu.VMEM((outer, inner) + block, jnp.float32),
             pltpu.VMEM((outer, inner) + block, jnp.float32),
             pltpu.VMEM((spread_by, outer) + block, jnp.float32),
             pltpu.VMEM((n,) + block, jnp.float32),
+            dma,
+            dma,
             dma,
         ]
         + [dma((outer, inner))] * 8

time: 23.7 us -> 23.2 us (0.979)
  Pallas kernels: 22.8 us -> 22.2 us
    pallas_call x1, Pallas kernels: 22.8 us -> 22.2 us  [on_device(): pl.pallas_call(functools.partial(reduce_kernel, n, outer, inner, spread_b...]
where the time goes in v4:
time: 23.2 us; the launch traced here: 23 us
  Pallas kernels  22.2 us (96%)
  local copies, waits for them, and re-layouts  0.8 us (3%)
    pallas_call x1, Pallas kernels, on_device(): pl.pallas_call(functools.partial(reduce_kernel, n, outer, inner, spread_b...  22.2 us
    unnamed x1, local copies, waits for them, and re-layouts  0.8 us

profile of v4, /device:TPU:0, one launch (start us, length us, event | category | flops | bytes accessed | tf_op | source)
XLA Modules:
  0.0 23.0 jit_solution(2268769340365453106)
XLA Ops:
  0.0 22.2 %reduce_all.1 = f32[2,8,64,128]{3,2,1,0:T(8,128)S(1)} custom-call(s32[2,8]{1,0:T(2,128)} %table_in.1, s32[2]{0:T(128)} %coefs_in.1, f32[2,8,64,128]{3,2,1,0:T(8,128)} %grids.1), custom_call_target="tpu_custom_call" | custom-call | tf_op jit(solution)/shard_map/reduce_all/pallas_call | solution.py:230
  22.2 0.8 %copy.5 = f32[2,8,64,128]{3,2,1,0:T(8,128)} copy(f32[2,8,64,128]{3,2,1,0:T(8,128)S(1)} %reduce_all.1) | data formatting | bytes 1048576
